TPU v7x, 32 devices: a whole 2x2x4 slice. The times are simulated.
32 devices in a mesh: fsdp: 8 (over z, x), tp: 4 (over y, core).
Axes of the slice: x: 2, y: 2, z: 4, core: 2. Of those that a mesh axis runs over, the one named last changes fastest.
Arguments:
- master: float32 [256, 8192], P('fsdp', 'tp'), may hold values from -0.0625 to 0.0625
- first_moment: float32 [256, 8192], P('fsdp', 'tp'), may hold values from -0.008286407 to 0.008286407
- second_moment: float32 [256, 8192], P('fsdp', 'tp'), may hold values from 2.3841858e-07 to 9.536743e-06
- gradients: float32 [256, 8192], P('fsdp', 'tp'), as said below
- step_count: int32 [1], replicated, may hold values from 1 to 8
- tile_round: int32 [32], replicated, may hold values from 0 to 3, as said below
Outputs:
- new_master: float32 [256, 8192], P('fsdp', 'tp')
- new_first: float32 [256, 8192], P('fsdp', 'tp')
- new_second: float32 [256, 8192], P('fsdp', 'tp')
- weights: bfloat16 [256, 8192], P(None, 'tp')
Inputs may be any that keep to these rules, and one draw needn't show every extreme that they name: `tile_round`: each aligned block of 4 entries (the tiles of one index of fsdp) holds every round number 0 to 3 exactly once. `gradients`: exactly one entry has magnitude 1000 or more; every other entry has magnitude under 100, and in every round without that entry the sum of squares is under 1e5.
All inputs are finite; a program needn't handle non-finite values.
Results may differ from a plain program's by a relative error of at most 0.001.
Values may be sent and summed in bfloat16 or wider, within the bound.
A program may use at most 64 MiB of HBM per device.

v0:
```python
import jax
import jax.numpy as jnp
from jax import lax
from jax.sharding import PartitionSpec as P

ROUNDS = 4


beta_one = 0.9
beta_two = 0.95
adam_epsilon = 1e-08
learning_rate = 0.01
weight_decay = 0.1
clip_norm = 1.0
square_limit = 1000000.0


def local(master, first_moment, second_moment, gradients, step_count, tile_round):
    row_count, columns = master.shape
    tile_rows = row_count // ROUNDS
    shaped = (ROUNDS, tile_rows, columns)
    params = master.reshape(shaped)
    moment_one = first_moment.reshape(shaped)
    moment_two = second_moment.reshape(shaped)
    grads = gradients.reshape(shaped)
    mine = lax.dynamic_slice_in_dim(tile_round, lax.axis_index("fsdp") * ROUNDS, ROUNDS)
    slot_ids = jnp.arange(ROUNDS, dtype=jnp.int32)
    places = [jnp.sum(jnp.where(mine == round_index, slot_ids, 0)) for round_index in range(ROUNDS)]
    grad_tiles = [
        lax.dynamic_index_in_dim(grads, places[round_index], 0, keepdims=False)
        for round_index in range(ROUNDS)
    ]
    squares = [jnp.sum(piece * piece) for piece in grad_tiles]
    totals = lax.psum(jnp.stack(squares), ("fsdp", "tp"))
    total_list = [totals[round_index] for round_index in range(ROUNDS)]
    broken_list = [totals[round_index] >= square_limit for round_index in range(ROUNDS)]
    steps = step_count[0].astype(jnp.float32)
    correct_one = 1.0 - jnp.power(jnp.float32(beta_one), steps)
    correct_two = 1.0 - jnp.power(jnp.float32(beta_two), steps)
    out_p, out_m, out_v = (params, moment_one, moment_two)
    for round_index in range(ROUNDS):
        where_at = places[round_index]
        old_p = lax.dynamic_index_in_dim(params, where_at, 0, keepdims=False)
        old_m = lax.dynamic_index_in_dim(moment_one, where_at, 0, keepdims=False)
        old_v = lax.dynamic_index_in_dim(moment_two, where_at, 0, keepdims=False)
        scale = jnp.minimum(
            jnp.float32(1.0), clip_norm / (jnp.sqrt(total_list[round_index]) + 1e-06)
        )
        clipped = grad_tiles[round_index] * scale
        moment_new = beta_one * old_m + (1.0 - beta_one) * clipped
        second_new = beta_two * old_v + (1.0 - beta_two) * clipped * clipped
        ratio = moment_new / correct_one / (jnp.sqrt(second_new / correct_two) + adam_epsilon)
        param_new = old_p - learning_rate * (ratio + weight_decay * old_p)
        keeping = broken_list[round_index]
        param_new = jnp.where(keeping, old_p, param_new)
        moment_new = jnp.where(keeping, old_m, moment_new)
        second_new = jnp.where(keeping, old_v, second_new)
        out_p = lax.dynamic_update_index_in_dim(out_p, param_new, where_at, 0)
        out_m = lax.dynamic_update_index_in_dim(out_m, moment_new, where_at, 0)
        out_v = lax.dynamic_update_index_in_dim(out_v, second_new, where_at, 0)
    new_master = out_p.reshape(row_count, columns)
    weights = lax.all_gather(new_master.astype(jnp.bfloat16), "fsdp", axis=0, tiled=True)
    return (
        new_master,
        out_m.reshape(row_count, columns),
        out_v.reshape(row_count, columns),
        weights,
    )


def solution(mesh):
    return jax.shard_map(
        local,
        mesh=mesh,
        in_specs=(P("fsdp", "tp"), P("fsdp", "tp"), P("fsdp", "tp"), P("fsdp", "tp"), P(), P()),
        out_specs=(P("fsdp", "tp"), P("fsdp", "tp"), P("fsdp", "tp"), P(None, "tp")),
        check_vma=False,
    )
```

profile of v0, /device:TPU:0, one launch (start us, length us, event | category | flops | bytes accessed | tf_op | source)
XLA Modules:
  0.0 123.5 jit_solution(17541143650168764831)
XLA Ops:
  7.2 0.0 copy-start.4
  7.2 0.0 all-gather.2.cloned.1.call-start
  7.2 1.4 %fusion.9 = (s32[]{:T(128)}, s32[]{:T(128)}, s32[]{:T(128)}, s32[]{:T(128)}) fusion(s32[32]{0:T(128)} %param.11, s32[]{:T(128)S(6)} %select_n.124), kind=kLoop, calls=%fused_computation.37 | loop fusion | flops 44 | bytes 36 | tf_op jit(solution)/shard_map/reduce_sum | solution.py:28
  16.4 1.6 %multiply_reduce_fusion.3 = (f32[]{:T(128)}, f32[]{:T(128)}, f32[]{:T(128)}, f32[]{:T(128)}) fusion(f32[4,8,2048]{2,1,0:T(8,128)} %bitcast.22, s32[]{:T(128)S(6)} %select_n.126, s32[]{:T(128)S(6)} %select_n.132, s32[]{:T(128)S(6)} %select_n.130, s32[]{:T(128)S(6)} %select_n.128), kind=kLoop, calls=%fused_computation.31 | loop fusion | flops 131068 | bytes 262176 | tf_op jit(solution)/shard_map/reduce_sum | solution.py:33
  18.0 2.7 %pad_maximum_fusion = f32[4]{0:T(128)S(1)} fusion(f32[1]{0:T(128)} %bitcast.5, f32[1]{0:T(128)} %bitcast.4, f32[1]{0:T(128)} %bitcast.3, f32[1]{0:T(128)} %bitcast.2), kind=kLoop, calls=%fused_computation.40 | loop fusion | flops 12 | bytes 32 | tf_op jit(solution)/shard_map/stack | solution.py:34
  20.7 41.9 %psum.7 = f32[4]{0:T(128)S(1)} all-reduce(f32[4]{0:T(128)S(1)} %pad_maximum_fusion), channel_id=1, replica_groups=mesh['fsdp'=8,'tp'=4] {'fsdp','tp'}, use_global_device_ids=true, to_apply=%region_8.9 | all-reduce | flops 4 | bytes 32 | tf_op jit(solution)/shard_map/psum | solution.py:34
  62.6 0.6 fusion.12
  69.4 0.0 copy-done.4
  69.5 0.0 copy-start.3
  69.5 0.9 copy-done.3
  70.4 0.9 copy-done.1
  71.4 0.9 copy-done
  72.3 0.1 select_dynamic-update-slice_fusion.2
  72.4 0.1 select_dynamic-update-slice_fusion.1
  72.5 0.1 select_dynamic-update-slice_fusion
  72.6 0.0 copy-start.6
  72.7 0.1 select_dynamic-update-slice_fusion.4
  72.8 0.5 copy-done.6
  73.3 0.7 bitcast_convert_fusion
  74.1 0.0 all-gather.2.cloned.1.call-update
  74.1 0.0 copy-done.2
  74.1 0.1 copy-done.5
  74.2 40.1 %all-gather.2.cloned.1.call-done = bf16[256,2048]{1,0:T(8,128)(2,1)} async-done(((bf16[32,2048]{1,0:T(8,128)(2,1)}), bf16[256,2048]{1,0:T(8,128)(2,1)}) %all-gather.2.cloned.1.call-update) | async-done | bytes 1048592 | tf_op jit(solution)/shard_map/all_gather | solution.py:62
  114.3 2.3 %copy.24 = bf16[256,2048]{1,0:T(8,128)(2,1)} copy(bf16[256,2048]{1,0:T(8,128)(2,1)} %all-gather.2.cloned.1.call-done) | data formatting | bytes 2097152
  (10 shorter events, 0.1 us)
Async XLA Ops:
  7.2 62.3 %copy-start.4 = (f32[32,2048]{1,0:T(8,128)S(1)}, f32[32,2048]{1,0:T(8,128)}, u32[]{:S(2)}) copy-start(f32[32,2048]{1,0:T(8,128)} %param.6) | copy-start | bytes 786436
  7.2 107.1 %all-gather.2.cloned.1.call-start = ((), (), s32[]{:S(2)}) async-start(), calls=%async_computation | async-start | bytes 1179648 | tf_op jit(solution)/shard_map/all_gather | solution.py:62
  69.5 1.0 copy-start.3
  70.4 0.9 copy-start.1
  71.4 0.9 copy-start
  72.6 0.7 copy-start.6
  73.3 0.7 copy-start.2
  73.3 0.8 copy-start.5
Sparse Core Ops, SparseCore 0:
  74.2 40.0 all-gather.1
where the time goes:
time: 124 us; the launch traced here: 123 us
  blocking collectives  41.9 us (34%)
  waiting for transfers between devices  40.2 us (32%)
  between operations  28.1 us (23%)
  other arithmetic  6.84 us (6%)
  local copies, waits for them, and re-layouts  6.36 us (5%)
    psum x1, blocking collectives, local(): totals = lax.psum(jnp.stack(squares), ('fsdp', 'tp'))  41.9 us
    all_gather x1, waiting for transfers between devices, local(): lax.all_gather(new_master.astype(jnp.bfloat16), 'fsdp', axis=0, tiled=True)  40.1 us
    unnamed x18, local copies, waits for them, and re-layouts  5.77 us
    another operation x1, other arithmetic, local(): totals = lax.psum(jnp.stack(squares), ('fsdp', 'tp'))  2.66 us
  transfers between devices with their start and end apart: 1, of which 1 were waited for; matrix products, arithmetic and copies ran while one was open for 0% of the time, Pallas kernels for 0%

commit v1 on v0

v1 whole, which is shorter than its diff:
```python
import functools

import jax
import jax.numpy as jnp
from jax import lax
from jax.experimental import pallas as pl
from jax.experimental.pallas import tpu as pltpu
from jax.sharding import PartitionSpec as P

ROUNDS = 4
LANES = 128
MESH = pl.DeviceIdType.MESH

beta_one = 0.9
beta_two = 0.95
adam_epsilon = 1e-08
learning_rate = 0.01
weight_decay = 0.1
clip_norm = 1.0
square_limit = 1000000.0


def plan(fsdp, columns):
    if fsdp > 16 or columns % (16 * LANES):
        return [(0, columns, False)]
    unit = columns // 16
    chunks, start = [], 0
    for index, units in enumerate((3, 3, 3, 3, 4)):
        chunks.append((start, units * unit, index == 0))
        start += units * unit
    return chunks


def kernel(fsdp, tp, chunks, g_hbm, p_hbm, m_hbm, v_hbm, step_ref, round_ref,
           p_out, m_out, v_out, w_out,
           g_ref, p_ref, m_ref, v_ref, own_a, slots_a, own_b, slots_b,
           load_sem, sa_sem, ra_sem, sb_sem, rb_sem, up_sem, down_sem, side_sem, recv_sem):
    line = fsdp // 2
    f = lax.axis_index("fsdp")
    t = lax.axis_index("tp")
    a = f // 2
    b = f % 2
    rows, columns = g_ref.shape
    tile = rows // ROUNDS

    group = [(db, dt) for db in range(2) for dt in range(tp) if (db, dt) != (0, 0)]

    def peer_a(db, dt):
        return (a * 2 + (b + db) % 2, (t + dt) % tp)

    def peer_b(d):
        return (((a + d) % line) * 2 + b, t)

    loads = [pltpu.make_async_copy(src, dst, load_sem.at[i]) for i, (src, dst) in enumerate(
        ((g_hbm, g_ref), (p_hbm, p_ref), (m_hbm, m_ref), (v_hbm, v_ref)))]
    loads[0].start()
    barrier = pltpu.get_barrier_semaphore()
    for d in range(1, line):
        pl.semaphore_signal(barrier, inc=1, device_id=peer_b(d), device_id_type=MESH)
    for db, dt in group:
        pl.semaphore_signal(barrier, inc=1, device_id=peer_a(db, dt), device_id_type=MESH)
    for load in loads[1:]:
        load.start()

    row_ids = lax.broadcasted_iota(jnp.int32, (8, LANES), 0)
    mine = [round_ref[f * ROUNDS + k] for k in range(ROUNDS)]
    loads[0].wait()
    payload = jnp.zeros((8, LANES), jnp.float32)
    for k in range(ROUNDS):
        part = jnp.zeros((tile, LANES), jnp.float32)
        for c in range(columns // LANES):
            piece = g_ref[k * tile:(k + 1) * tile, c * LANES:(c + 1) * LANES]
            part = part + piece * piece
        part = jnp.sum(part, axis=0, keepdims=True)
        payload = payload + jnp.where(row_ids == mine[k], part, 0.0)
    own_a[...] = payload
    pl.semaphore_wait(barrier, len(group) + line - 1)

    sends_a = []
    for i, (db, dt) in enumerate(group):
        sends_a.append(pltpu.make_async_remote_copy(
            src_ref=own_a, dst_ref=slots_a.at[i], send_sem=sa_sem.at[i], recv_sem=ra_sem.at[i],
            device_id=peer_a(db, dt), device_id_type=MESH))
        sends_a[-1].start()
    for load in loads[1:]:
        load.wait()
    steps = jnp.full((1, LANES), step_ref[0].astype(jnp.float32), jnp.float32)
    inverse_one = 1.0 / (1.0 - jnp.exp(steps * jnp.log(jnp.float32(beta_one))))
    inverse_two = 1.0 / (1.0 - jnp.exp(steps * jnp.log(jnp.float32(beta_two))))
    inverse_one = inverse_one[:, :1]
    inverse_two = inverse_two[:, :1]
    total = payload
    for i, copy in enumerate(sends_a):
        copy.wait_recv()
        total = total + slots_a[i]
    own_b[...] = total
    sends_b = []
    for d in range(1, line):
        sends_b.append(pltpu.make_async_remote_copy(
            src_ref=own_b, dst_ref=slots_b.at[d - 1], send_sem=sb_sem.at[d - 1], recv_sem=rb_sem.at[d - 1],
            device_id=peer_b(d), device_id_type=MESH))
        sends_b[-1].start()
    for d, copy in enumerate(sends_b):
        copy.wait_recv()
        total = total + slots_b[d]

    scales, keeps = [], []
    for k in range(ROUNDS):
        picked = jnp.sum(jnp.where(row_ids == mine[k], total, 0.0), axis=0, keepdims=True)
        picked = jnp.sum(picked, axis=1, keepdims=True)
        keeps.append(picked >= square_limit)
        scales.append(jnp.minimum(1.0, clip_norm / (jnp.sqrt(picked) + 1e-06)))

    def block_of(row, c):
        start, width, _ = chunks[c]
        return w_out.at[pl.ds(pl.multiple_of(row * rows, rows), rows), pl.ds(start, width)]

    def send(row, c, sems, target):
        return pltpu.make_async_remote_copy(
            src_ref=block_of(row, c), dst_ref=block_of(row, c), send_sem=sems.at[row, c],
            recv_sem=recv_sem.at[row, c], device_id=(target, t), device_id_type=MESH)

    side = a * 2 + (1 - b)
    above, below = a < line - 1, a > 0

    def up(row, c):
        return send(row, c, up_sem, f + 2)

    def down(row, c):
        return send(row, c, down_sem, f - 2)

    def across(row, c):
        return send(row, c, side_sem, side)

    def when_do(condition, make, method):
        @pl.when(condition)
        def _():
            getattr(make(), method)()

    sent = []

    def go(condition, make):
        when_do(condition, make, "start")
        sent.append((condition, make))

    always = a >= 0
    for c, (start, width, first) in enumerate(chunks):
        for k in range(ROUNDS):
            at = (slice(k * tile, (k + 1) * tile), slice(start, start + width))
            old_p, old_m, old_v = p_ref[at], m_ref[at], v_ref[at]
            clipped = g_ref[at] * scales[k]
            moment = beta_one * old_m + (1.0 - beta_one) * clipped
            second = beta_two * old_v + (1.0 - beta_two) * clipped * clipped
            ratio = moment * inverse_one / (jnp.sqrt(second * inverse_two) + adam_epsilon)
            param = old_p - learning_rate * (ratio + weight_decay * old_p)
            param = jnp.where(keeps[k], old_p, param)
            p_out[at] = param
            m_out[at] = jnp.where(keeps[k], old_m, moment)
            v_out[at] = jnp.where(keeps[k], old_v, second)
        own_rows = pl.ds(pl.multiple_of(f * rows, rows), rows)
        w_out[own_rows, start:start + width] = p_out[:, start:start + width].astype(jnp.bfloat16)
        go(always, functools.partial(across, f, c))
        go(above, functools.partial(up, f, c))
        go(below, functools.partial(down, f, c))

    for c, (_, _, first) in enumerate(chunks):
        if first:
            across(side, c).wait_recv()
            go(above, functools.partial(up, side, c))
            go(below, functools.partial(down, side, c))

    for d in range(1, line):
        for c, (_, _, first) in enumerate(chunks):
            for from_below in (True, False):
                inside = (a >= d) if from_below else (a + d <= line - 1)
                onward = above if from_below else below
                shift = -2 * d if from_below else 2 * d
                for adopted in ((False, True) if first else (False,)):
                    row = (side if adopted else f) + shift
                    make = functools.partial(up if from_below else down, row, c)
                    when_do(inside, make, "wait_recv")
                    go(jnp.logical_and(inside, onward), make)
                    if not first:
                        go(inside, functools.partial(across, row, c))

    for c, (_, _, first) in enumerate(chunks):
        if not first:
            across(side, c).wait_recv()
    for d in range(1, line):
        for c, (_, _, first) in enumerate(chunks):
            if not first:
                when_do(a >= d, functools.partial(across, side - 2 * d, c), "wait_recv")
                when_do(a + d <= line - 1, functools.partial(across, side + 2 * d, c), "wait_recv")

    for copy in sends_a + sends_b:
        copy.wait_send()
    for condition, make in sent:
        when_do(condition, make, "wait_send")


def solution(mesh):
    fsdp, tp = mesh.shape["fsdp"], mesh.shape["tp"]

    def local(master, first_moment, second_moment, gradients, step_count, tile_round):
        rows, columns = master.shape
        chunks = plan(fsdp, columns)
        count = len(chunks)
        line = fsdp // 2
        shape = jax.ShapeDtypeStruct((rows, columns), jnp.float32)
        sems = pltpu.SemaphoreType.DMA
        block = pltpu.VMEM((rows, columns), jnp.float32)
        p, m, v, w = pl.pallas_call(
            functools.partial(kernel, fsdp, tp, chunks),
            out_shape=(shape, shape, shape, jax.ShapeDtypeStruct((fsdp * rows, columns), jnp.bfloat16)),
            in_specs=[pl.BlockSpec(memory_space=pltpu.HBM)] * 4 + [pl.BlockSpec(memory_space=pltpu.SMEM)] * 2,
            out_specs=[pl.BlockSpec(memory_space=pltpu.VMEM)] * 4,
            scratch_shapes=[
                block, block, block, block,
                pltpu.VMEM((8, LANES), jnp.float32),
                pltpu.VMEM((2 * tp - 1, 8, LANES), jnp.float32),
                pltpu.VMEM((8, LANES), jnp.float32),
                pltpu.VMEM((line - 1, 8, LANES), jnp.float32),
                sems((4,)), sems((2 * tp - 1,)), sems((2 * tp - 1,)), sems((line - 1,)), sems((line - 1,)),
                sems((fsdp, count)), sems((fsdp, count)), sems((fsdp, count)), sems((fsdp, count)),
            ],
            compiler_params=pltpu.CompilerParams(
                collective_id=0, has_side_effects=True, vmem_limit_bytes=40 * 1024 * 1024),
        )(gradients, master, first_moment, second_moment, step_count, tile_round)
        return p, m, v, w

    return jax.shard_map(
        local,
        mesh=mesh,
        in_specs=(P("fsdp", "tp"), P("fsdp", "tp"), P("fsdp", "tp"), P("fsdp", "tp"), P(), P()),
        out_specs=(P("fsdp", "tp"), P("fsdp", "tp"), P("fsdp", "tp"), P(None, "tp")),
        check_vma=False,
    )
```

time: 124 us -> 39.1 us (0.32)
  blocking collectives: 41.9 us -> 0 us
  waiting for transfers between devices: 40.2 us -> 0 us
  Pallas kernels: 0 us -> 30.6 us
  between operations: 28.1 us -> 1.33 us
  other arithmetic: 6.84 us -> 0 us
    psum x1 -> x0, blocking collectives: 41.9 us -> none  [local(): totals = lax.psum(jnp.stack(squares), ('fsdp', 'tp'))]
    all_gather x1 -> x0, waiting for transfers between devices: 40.1 us -> none  [local(): lax.all_gather(new_master.astype(jnp.bfloat16), 'fsdp', axis=0, tiled=True)]
    pallas_call x0 -> x1, Pallas kernels: none -> 30.6 us  [local(): pl.pallas_call(functools.partial(kernel, fsdp, tp, chunks), out_shape=(sh...]
    reduce_sum x2 -> x0, other arithmetic: 3.01 us -> none  [the longest x1 1.58 us: local(): squares = [jnp.sum(piece * piece) for piece in grad_tiles]]
    another operation x1 -> x0, other arithmetic: 2.66 us -> none  [local(): totals = lax.psum(jnp.stack(squares), ('fsdp', 'tp'))]
    unnamed x18 -> x14, local copies, waits for them, and re-layouts: 5.77 us -> 6.87 us
  transfers between devices with their start and end apart: 1 -> 0, of which waited for: 1 -> 0; matrix products, arithmetic and copies ran while one was open for 0% -> 0% of each run, Pallas kernels for 0% -> 0%
where the time goes in v1:
time: 39.1 us; the launch traced here: 38.9 us
  Pallas kernels  30.6 us (78%)
  local copies, waits for them, and re-layouts  6.87 us (18%)
  between operations  1.33 us (3%)
    pallas_call x1, Pallas kernels, local(): pl.pallas_call(functools.partial(kernel, fsdp, tp, chunks), out_shape=(sh...  30.6 us
    unnamed x14, local copies, waits for them, and re-layouts  6.87 us

profile of v1, /device:TPU:0, one launch (start us, length us, event | category | flops | bytes accessed | tf_op | source)
XLA Modules:
  0.0 38.9 jit_solution(113456957904209291)
XLA Ops:
  0.6 0.0 copy-start.4
  1.3 0.0 copy-done.4
  1.3 0.0 copy-start
  1.3 0.9 %copy-done = f32[32,2048]{1,0:T(8,128)S(1)} copy-done((f32[32,2048]{1,0:T(8,128)S(1)}, f32[32,2048]{1,0:T(8,128)}, u32[]{:S(2)}) %copy-start) | copy-done | bytes 262168
  2.3 0.0 copy-start.1
  2.3 0.9 %copy-done.1 = f32[32,2048]{1,0:T(8,128)S(1)} copy-done((f32[32,2048]{1,0:T(8,128)S(1)}, f32[32,2048]{1,0:T(8,128)}, u32[]{:S(2)}) %copy-start.1) | copy-done | bytes 262168
  3.2 0.0 copy-start.2
  3.2 0.9 %copy-done.2 = f32[32,2048]{1,0:T(8,128)S(1)} copy-done((f32[32,2048]{1,0:T(8,128)S(1)}, f32[32,2048]{1,0:T(8,128)}, u32[]{:S(2)}) %copy-start.2) | copy-done | bytes 262168
  4.2 0.0 copy-start.3
  4.2 0.9 %copy-done.3 = f32[32,2048]{1,0:T(8,128)S(1)} copy-done((f32[32,2048]{1,0:T(8,128)S(1)}, f32[32,2048]{1,0:T(8,128)}, u32[]{:S(2)}) %copy-start.3) | copy-done | bytes 262168
  5.1 30.6 %shard_map.93 = (f32[32,2048]{1,0:T(8,128)S(1)}, f32[32,2048]{1,0:T(8,128)S(1)}, f32[32,2048]{1,0:T(8,128)S(1)}, bf16[256,2048]{1,0:T(8,128)(2,1)S(1)}) custom-call(f32[32,2048]{1,0:T(8,128)S(1)} %copy-done, f32[32,2048]{1,0:T(8,128)S(1)} %copy-done.1, f32[32,2048]{1,0:T(8,128)S(1)} %copy-done.2, f32[32,2048]{1,0:T(8,128)S(1)} %copy-done.3, ...), custom_call_target="tpu_custom_call" | custom-call | tf_op jit(solution)/shard_map/pallas_call | solution.py:212
  35.8 0.7 %copy.15 = f32[32,2048]{1,0:T(8,128)} copy(f32[32,2048]{1,0:T(8,128)S(1)} %get-tuple-element.8) | data formatting | bytes 524288
  36.5 0.7 %copy.16 = f32[32,2048]{1,0:T(8,128)} copy(f32[32,2048]{1,0:T(8,128)S(1)} %get-tuple-element.9) | data formatting | bytes 524288
  37.2 0.7 %copy.17 = f32[32,2048]{1,0:T(8,128)} copy(f32[32,2048]{1,0:T(8,128)S(1)} %get-tuple-element.10) | data formatting | bytes 524288
  37.9 1.0 %copy.18 = bf16[256,2048]{1,0:T(8,128)(2,1)} copy(bf16[256,2048]{1,0:T(8,128)(2,1)S(1)} %get-tuple-element.11) | data formatting | bytes 2097152
Async XLA Ops:
  0.6 0.7 %copy-start.4 = (s32[32]{0:T(128)S(1)}, s32[32]{0:T(128)}, u32[]{:S(2)}) copy-start(s32[32]{0:T(128)} %round_ref.1) | copy-start | bytes 388
  1.3 1.0 %copy-start = (f32[32,2048]{1,0:T(8,128)S(1)}, f32[32,2048]{1,0:T(8,128)}, u32[]{:S(2)}) copy-start(f32[32,2048]{1,0:T(8,128)} %g_hbm.1) | copy-start | bytes 786436
  2.3 0.9 %copy-start.1 = (f32[32,2048]{1,0:T(8,128)S(1)}, f32[32,2048]{1,0:T(8,128)}, u32[]{:S(2)}) copy-start(f32[32,2048]{1,0:T(8,128)} %p_hbm.1) | copy-start | bytes 786436
  3.2 0.9 %copy-start.2 = (f32[32,2048]{1,0:T(8,128)S(1)}, f32[32,2048]{1,0:T(8,128)}, u32[]{:S(2)}) copy-start(f32[32,2048]{1,0:T(8,128)} %m_hbm.1) | copy-start | bytes 786436
  4.2 0.9 %copy-start.3 = (f32[32,2048]{1,0:T(8,128)S(1)}, f32[32,2048]{1,0:T(8,128)}, u32[]{:S(2)}) copy-start(f32[32,2048]{1,0:T(8,128)} %v_hbm.1) | copy-start | bytes 786436

commit v2 on v1

--- a/solution.py
+++ b/solution.py
@@ -25,16 +25,16 @@
         return [(0, columns, False)]
     unit = columns // 16
     chunks, start = [], 0
-    for index, units in enumerate((3, 3, 3, 3, 4)):
-        chunks.append((start, units * unit, index == 0))
+    for index, units in enumerate((4, 4, 4, 4)):
+        chunks.append((start, units * unit, False))
         start += units * unit
     return chunks
 
 
-def kernel(fsdp, tp, chunks, g_hbm, p_hbm, m_hbm, v_hbm, step_ref, round_ref,
+def kernel(fsdp, tp, chunks, g_hbm, p_hbm, m_hbm, v_hbm, step_hbm, round_hbm,
            p_out, m_out, v_out, w_out,
            g_ref, p_ref, m_ref, v_ref, own_a, slots_a, own_b, slots_b,
-           load_sem, sa_sem, ra_sem, sb_sem, rb_sem, up_sem, down_sem, side_sem, recv_sem):
+           step_ref, round_ref, load_sem, sa_sem, ra_sem, sb_sem, rb_sem, up_sem, down_sem, side_sem, recv_sem):
     line = fsdp // 2
     f = lax.axis_index("fsdp")
     t = lax.axis_index("tp")
@@ -52,7 +52,8 @@
         return (((a + d) % line) * 2 + b, t)
 
     loads = [pltpu.make_async_copy(src, dst, load_sem.at[i]) for i, (src, dst) in enumerate(
-        ((g_hbm, g_ref), (p_hbm, p_ref), (m_hbm, m_ref), (v_hbm, v_ref)))]
+        ((g_hbm, g_ref), (round_hbm, round_ref), (step_hbm, step_ref),
+         (p_hbm, p_ref), (m_hbm, m_ref), (v_hbm, v_ref)))]
     loads[0].start()
     barrier = pltpu.get_barrier_semaphore()
     for d in range(1, line):
@@ -63,6 +64,7 @@
         load.start()
 
     row_ids = lax.broadcasted_iota(jnp.int32, (8, LANES), 0)
+    loads[1].wait()
     mine = [round_ref[f * ROUNDS + k] for k in range(ROUNDS)]
     loads[0].wait()
     payload = jnp.zeros((8, LANES), jnp.float32)
@@ -82,7 +84,7 @@
             src_ref=own_a, dst_ref=slots_a.at[i], send_sem=sa_sem.at[i], recv_sem=ra_sem.at[i],
             device_id=peer_a(db, dt), device_id_type=MESH))
         sends_a[-1].start()
-    for load in loads[1:]:
+    for load in loads[2:]:
         load.wait()
     steps = jnp.full((1, LANES), step_ref[0].astype(jnp.float32), jnp.float32)
     inverse_one = 1.0 / (1.0 - jnp.exp(steps * jnp.log(jnp.float32(beta_one))))
@@ -170,18 +172,18 @@
             go(below, functools.partial(down, side, c))
 
     for d in range(1, line):
-        for c, (_, _, first) in enumerate(chunks):
+        passing = [(False, c) for c in range(len(chunks))]
+        passing += [(True, c) for c, (_, _, first) in enumerate(chunks) if first]
+        for adopted, c in passing:
             for from_below in (True, False):
                 inside = (a >= d) if from_below else (a + d <= line - 1)
                 onward = above if from_below else below
-                shift = -2 * d if from_below else 2 * d
-                for adopted in ((False, True) if first else (False,)):
-                    row = (side if adopted else f) + shift
-                    make = functools.partial(up if from_below else down, row, c)
-                    when_do(inside, make, "wait_recv")
-                    go(jnp.logical_and(inside, onward), make)
-                    if not first:
-                        go(inside, functools.partial(across, row, c))
+                row = (side if adopted else f) + (-2 * d if from_below else 2 * d)
+                make = functools.partial(up if from_below else down, row, c)
+                when_do(inside, make, "wait_recv")
+                go(jnp.logical_and(inside, onward), make)
+                if not (adopted or chunks[c][2]):
+                    go(inside, functools.partial(across, row, c))
 
     for c, (_, _, first) in enumerate(chunks):
         if not first:
@@ -196,6 +198,15 @@
         copy.wait_send()
     for condition, make in sent:
         when_do(condition, make, "wait_send")
+
+
+def put_out(*refs):
+    sources, targets, sem = refs[:4], refs[4:8], refs[8]
+    copies = [pltpu.make_async_copy(src, dst, sem.at[i]) for i, (src, dst) in enumerate(zip(sources, targets))]
+    for copy in reversed(copies):
+        copy.start()
+    for copy in copies:
+        copy.wait()
 
 
 def solution(mesh):
@@ -212,7 +223,7 @@
         p, m, v, w = pl.pallas_call(
             functools.partial(kernel, fsdp, tp, chunks),
             out_shape=(shape, shape, shape, jax.ShapeDtypeStruct((fsdp * rows, columns), jnp.bfloat16)),
-            in_specs=[pl.BlockSpec(memory_space=pltpu.HBM)] * 4 + [pl.BlockSpec(memory_space=pltpu.SMEM)] * 2,
+            in_specs=[pl.BlockSpec(memory_space=pltpu.HBM)] * 4 + [pl.BlockSpec(memory_space=pl.ANY)] * 2,
             out_specs=[pl.BlockSpec(memory_space=pltpu.VMEM)] * 4,
             scratch_shapes=[
                 block, block, block, block,
@@ -220,13 +231,23 @@
                 pltpu.VMEM((2 * tp - 1, 8, LANES), jnp.float32),
                 pltpu.VMEM((8, LANES), jnp.float32),
                 pltpu.VMEM((line - 1, 8, LANES), jnp.float32),
-                sems((4,)), sems((2 * tp - 1,)), sems((2 * tp - 1,)), sems((line - 1,)), sems((line - 1,)),
+                pltpu.SMEM(step_count.shape, jnp.int32), pltpu.SMEM(tile_round.shape, jnp.int32),
+                sems((6,)), sems((2 * tp - 1,)), sems((2 * tp - 1,)), sems((line - 1,)), sems((line - 1,)),
                 sems((fsdp, count)), sems((fsdp, count)), sems((fsdp, count)), sems((fsdp, count)),
             ],
             compiler_params=pltpu.CompilerParams(
                 collective_id=0, has_side_effects=True, vmem_limit_bytes=40 * 1024 * 1024),
-        )(gradients, master, first_moment, second_moment, step_count, tile_round)
-        return p, m, v, w
+        )(*[pltpu.with_memory_space_constraint(x, pltpu.HBM) for x in (
+            gradients, master, first_moment, second_moment)], step_count, tile_round)
+        results = (p, m, v, w)
+        return pl.pallas_call(
+            put_out,
+            out_shape=tuple(jax.ShapeDtypeStruct(x.shape, x.dtype) for x in results),
+            in_specs=[pl.BlockSpec(memory_space=pltpu.VMEM)] * 4,
+            out_specs=[pl.BlockSpec(memory_space=pltpu.HBM)] * 4,
+            scratch_shapes=[sems((4,))],
+            compiler_params=pltpu.CompilerParams(vmem_limit_bytes=1024 * 1024),
+        )(*results)
 
     return jax.shard_map(
         local,

time: 39.1 us -> 29.4 us (0.75)
  local copies, waits for them, and re-layouts: 6.87 us -> 0.01 us
  Pallas kernels: 30.6 us -> 27.9 us
    unnamed x14 -> x2, local copies, waits for them, and re-layouts: 6.87 us -> 0.01 us
    pallas_call x1, Pallas kernels: 30.6 us -> 26.7 us  [local(): pl.pallas_call(functools.partial(kernel, fsdp, tp, chunks), out_shape=(sh...]
    pallas_call x0 -> x1, Pallas kernels: none -> 1.26 us  [local(): pl.pallas_call(put_out, out_shape=tuple((jax.ShapeDtypeStruct(x.shape, x....]
where the time goes in v2:
time: 29.4 us; the launch traced here: 29.3 us
  Pallas kernels  27.9 us (95%)
  between operations  1.31 us (4%)
    pallas_call x1, Pallas kernels, local(): pl.pallas_call(functools.partial(kernel, fsdp, tp, chunks), out_shape=(sh...  26.7 us
    pallas_call x1, Pallas kernels, local(): pl.pallas_call(put_out, out_shape=tuple((jax.ShapeDtypeStruct(x.shape, x....  1.26 us

profile of v2, /device:TPU:0, one launch (start us, length us, event | category | flops | bytes accessed | tf_op | source)
XLA Modules:
  0.0 29.3 jit_solution(6206542588936389224)
XLA Ops:
  0.6 0.0 copy-start
  1.3 0.0 copy-done
  1.3 26.7 %shard_map.93 = (f32[32,2048]{1,0:T(8,128)S(1)}, f32[32,2048]{1,0:T(8,128)S(1)}, f32[32,2048]{1,0:T(8,128)S(1)}, bf16[256,2048]{1,0:T(8,128)(2,1)S(1)}) custom-call(f32[32,2048]{1,0:T(8,128)} %g_hbm.1, f32[32,2048]{1,0:T(8,128)} %p_hbm.1, f32[32,2048]{1,0:T(8,128)} %m_hbm.1, f32[32,2048]{1,0:T(8,128)} %v_hbm.1, s32[1]{0:T(128)S(6)} %copy.10.step_hbm, ...), custom_call_target="tpu_custom_call" | custom-call | tf_op jit(solution)/shard_map/pallas_call | solution.py:223
  28.0 1.3 %shard_map.94 = (f32[32,2048]{1,0:T(8,128)}, f32[32,2048]{1,0:T(8,128)}, f32[32,2048]{1,0:T(8,128)}, bf16[256,2048]{1,0:T(8,128)(2,1)}) custom-call(f32[32,2048]{1,0:T(8,128)S(1)} %get-tuple-element.8.refs_0_, f32[32,2048]{1,0:T(8,128)S(1)} %get-tuple-element.9.refs_1_, f32[32,2048]{1,0:T(8,128)S(1)} %get-tuple-element.10.refs_2_, ...), custom_call_target="tpu_custom_call" | custom-call | tf_op jit(solution)/shard_map/pallas_call | solution.py:243
Async XLA Ops:
  0.6 0.7 %copy-start = (s32[32]{0:T(128)S(1)}, s32[32]{0:T(128)}, u32[]{:S(2)}) copy-start(s32[32]{0:T(128)} %round_hbm.1) | copy-start | bytes 388

commit v3 on v2

--- a/solution.py
+++ b/solution.py
@@ -223,7 +223,7 @@
         p, m, v, w = pl.pallas_call(
             functools.partial(kernel, fsdp, tp, chunks),
             out_shape=(shape, shape, shape, jax.ShapeDtypeStruct((fsdp * rows, columns), jnp.bfloat16)),
-            in_specs=[pl.BlockSpec(memory_space=pltpu.HBM)] * 4 + [pl.BlockSpec(memory_space=pl.ANY)] * 2,
+            in_specs=[pl.BlockSpec(memory_space=pltpu.HBM)] * 4 + [pl.BlockSpec(memory_space=pl.ANY), pl.BlockSpec(memory_space=pltpu.HBM)],
             out_specs=[pl.BlockSpec(memory_space=pltpu.VMEM)] * 4,
             scratch_shapes=[
                 block, block, block, block,
@@ -238,7 +238,8 @@
             compiler_params=pltpu.CompilerParams(
                 collective_id=0, has_side_effects=True, vmem_limit_bytes=40 * 1024 * 1024),
         )(*[pltpu.with_memory_space_constraint(x, pltpu.HBM) for x in (
-            gradients, master, first_moment, second_moment)], step_count, tile_round)
+            gradients, master, first_moment, second_moment)], step_count,
+          pltpu.with_memory_space_constraint(tile_round, pltpu.HBM))
         results = (p, m, v, w)
         return pl.pallas_call(
             put_out,

time: 29.4 us -> 29.4 us (level)
  no operation moved by 1% of the time
where the time goes in v3:
time: 29.4 us; the launch traced here: 29.2 us
  Pallas kernels  27.9 us (95%)
  between operations  1.29 us (4%)
    pallas_call x1, Pallas kernels, local(): pl.pallas_call(functools.partial(kernel, fsdp, tp, chunks), out_shape=(sh...  26.7 us
    pallas_call x1, Pallas kernels, local(): pl.pallas_call(put_out, out_shape=tuple((jax.ShapeDtypeStruct(x.shape, x....  1.26 us

profile of v3, /device:TPU:0, one launch (start us, length us, event | category | flops | bytes accessed | tf_op | source)
XLA Modules:
  0.0 29.2 jit_solution(6777885024897820817)
XLA Ops:
  1.3 26.7 %shard_map.93 = (f32[32,2048]{1,0:T(8,128)S(1)}, f32[32,2048]{1,0:T(8,128)S(1)}, f32[32,2048]{1,0:T(8,128)S(1)}, bf16[256,2048]{1,0:T(8,128)(2,1)S(1)}) custom-call(f32[32,2048]{1,0:T(8,128)} %g_hbm.1, f32[32,2048]{1,0:T(8,128)} %p_hbm.1, f32[32,2048]{1,0:T(8,128)} %m_hbm.1, f32[32,2048]{1,0:T(8,128)} %v_hbm.1, s32[1]{0:T(128)S(6)} %copy.10.step_hbm, ...), custom_call_target="tpu_custom_call" | custom-call | tf_op jit(solution)/shard_map/pallas_call | solution.py:223
  28.0 1.3 %shard_map.94 = (f32[32,2048]{1,0:T(8,128)}, f32[32,2048]{1,0:T(8,128)}, f32[32,2048]{1,0:T(8,128)}, bf16[256,2048]{1,0:T(8,128)(2,1)}) custom-call(f32[32,2048]{1,0:T(8,128)S(1)} %get-tuple-element.8.refs_0_, f32[32,2048]{1,0:T(8,128)S(1)} %get-tuple-element.9.refs_1_, f32[32,2048]{1,0:T(8,128)S(1)} %get-tuple-element.10.refs_2_, ...), custom_call_target="tpu_custom_call" | custom-call | tf_op jit(solution)/shard_map/pallas_call | solution.py:244
